TPU v7x, 32 devices: a whole 2x2x4 slice. The times are simulated.
32 devices in a mesh: grp: 2 (over x), seq: 4 (over y, core), tp: 4 (over z).
Axes of the slice: x: 2, y: 2, z: 4, core: 2. Of those that a mesh axis runs over, the one named last changes fastest.
Arguments:
- hidden: bfloat16 [2, 1024, 4096], P('grp', 'seq'), may hold values from -72 to 72
- w_query: bfloat16 [4096, 2048], P('seq', 'tp'), may hold values from -0.09375 to 0.09375
- w_key: bfloat16 [4096, 2048], P('seq', 'tp'), may hold values from -0.09375 to 0.09375
- w_value: bfloat16 [4096, 2048], P('seq', 'tp'), may hold values from -0.09375 to 0.09375
- prompt_len: int32 [256], replicated, may hold values from 1 to 1024
- page_table: int32 [256, 32], replicated, may hold values from 0 to 63, all different within a row
Outputs:
- attended: bfloat16 [2, 1024, 2048], P('grp', 'seq', 'tp')
Inputs may be any that keep to these rules, and one draw needn't show every extreme that they name: `page_table`: every row lists 32 different pages; every page is listed by some row.
All inputs are finite; a program needn't handle non-finite values.
Results may differ from a plain program's by a relative error of at most 0.006.
The roundings to bfloat16 on the way count: a program that leaves them out, or rounds other values in their place, can miss the bound.
Values may be sent and summed in bfloat16 or wider, within the bound.
A program may use at most 128 MiB of HBM per device.

v0:
```python
import math

import jax
import jax.numpy as jnp
from jax import lax
from jax.sharding import PartitionSpec as P

HD = 128
PAGE = 16
STEPS = 4


NEG = -1e30


def from_behind(value, axis, steps):
    count = lax.axis_size(axis)
    first, last = (max(0, -steps), min(count, count - steps))
    return lax.ppermute(value, axis, [(source, source + steps) for source in range(first, last)])


def partial_attention(query, keys, values, allowed):
    rows = query.shape[0]
    heads = query.shape[1] // HD
    query_heads = query.reshape(rows, heads, HD)
    key_heads = keys.reshape(keys.shape[0], heads, HD)
    value_heads = values.reshape(values.shape[0], heads, HD)
    scores = jnp.einsum(
        "rhd,shd->hrs", query_heads, key_heads, preferred_element_type=jnp.float32
    ) * HD ** (-0.5)
    scores = jnp.where(allowed[None], scores, NEG)
    top = jnp.max(scores, axis=2)
    weights = jnp.where(allowed[None], jnp.exp(scores - top[:, :, None]), 0.0)
    total = jnp.sum(weights, axis=2)
    summed = jnp.einsum(
        "hrs,shd->rhd",
        weights.astype(jnp.bfloat16),
        value_heads,
        preferred_element_type=jnp.float32,
    )
    return (top, total, summed.reshape(rows, heads * HD))


def rescale(summed, factor):
    rows = summed.shape[0]
    heads = factor.shape[0]
    return (summed.reshape(rows, heads, HD) * factor.T[:, :, None]).reshape(rows, heads * HD)


def combine(first, second):
    top = jnp.maximum(first[0], second[0])
    early = jnp.exp(first[0] - top)
    later = jnp.exp(second[0] - top)
    return (
        top,
        first[1] * early + second[1] * later,
        rescale(first[2], early) + rescale(second[2], later),
    )


def finish(state):
    return rescale(state[2], 1.0 / state[1]).astype(jnp.bfloat16)


def row_mask(tables, lengths, key_pos):
    pages = key_pos // PAGE
    member = jnp.any(tables[:, :, None] == pages[None, None, :], axis=1)
    allowed = member & (key_pos[None, :] < lengths[:, None])
    return jnp.repeat(allowed, STEPS, axis=0)


def blocked(carry, keys, values, query, mask_of):
    count = keys.shape[0]
    block = math.gcd(count, 512)

    def one_block(state, offset):
        piece_keys = lax.dynamic_slice_in_dim(keys, offset, block, 0)
        piece_values = lax.dynamic_slice_in_dim(values, offset, block, 0)
        key_pos = offset + jnp.arange(block)
        return (
            combine(state, partial_attention(query, piece_keys, piece_values, mask_of(key_pos))),
            None,
        )

    offsets = jnp.arange(count // block) * block
    state, unused = lax.scan(one_block, carry, offsets)
    return state


def on_device(hidden, w_query, w_key, w_value, prompt_len, page_table):
    local = hidden[0]
    rows = local.shape[0]
    width = w_query.shape[1]
    heads = width // HD
    seq_index = lax.axis_index("seq")
    is_prompt = lax.axis_index("grp") == 0
    empty = jnp.zeros((rows, width), jnp.float32)
    piece = (
        lax.all_gather(w_query, "seq", axis=0, tiled=True),
        lax.all_gather(w_key, "seq", axis=0, tiled=True),
        lax.all_gather(w_value, "seq", axis=0, tiled=True),
    )
    projected = tuple(
        (jnp.dot(local, weight, preferred_element_type=jnp.float32) for weight in piece)
    )
    query, keys, values = [item.astype(jnp.bfloat16) for item in projected]
    positions = seq_index * rows + jnp.arange(rows)
    start_state = (
        jnp.full((heads, rows), NEG, jnp.float32),
        jnp.zeros((heads, rows), jnp.float32),
        empty,
    )
    given_keys, given_values = from_behind((keys, values), "grp", 1)
    cache_keys = jnp.where(is_prompt, keys, given_keys)
    cache_values = jnp.where(is_prompt, values, given_values)
    row_count = rows // STEPS
    own_tables = lax.dynamic_slice_in_dim(page_table, seq_index * row_count, row_count, 0)
    own_lengths = lax.dynamic_slice_in_dim(prompt_len, seq_index * row_count, row_count, 0)

    def mask_of(key_pos):
        causal = key_pos[None, :] <= positions[:, None]
        listed = row_mask(own_tables, own_lengths, key_pos)
        return jnp.where(is_prompt, causal, listed)

    piece = (
        lax.all_gather(cache_keys, "seq", axis=0, tiled=True),
        lax.all_gather(cache_values, "seq", axis=0, tiled=True),
    )
    state = blocked(start_state, piece[0], piece[1], query, mask_of)
    frame_row = positions // STEPS
    own_rows = (frame_row[:, None] == frame_row[None, :]) & (
        positions[None, :] <= positions[:, None]
    )
    fresh = partial_attention(query, keys, values, own_rows)
    prefill_out = finish(state)
    decode_out = finish(combine(state, fresh))
    return jnp.where(is_prompt, prefill_out, decode_out)[None]


def solution(mesh):
    return jax.shard_map(
        on_device,
        mesh=mesh,
        in_specs=(P("grp", "seq", None), P("seq", "tp"), P("seq", "tp"), P("seq", "tp"), P(), P()),
        out_specs=P("grp", "seq", "tp"),
        check_vma=False,
    )
```

profile of v0, /device:TPU:2, one launch (start us, length us, event | category | flops | bytes accessed | tf_op | source)
XLA Modules:
  0.0 202.8 jit_solution(16664680472872045981)
XLA Ops:
  8.8 35.8 %all-gather.6.cloned.1.call-done = bf16[4096,512]{1,0:T(8,128)(2,1)} async-done(((bf16[1024,512]{1,0:T(8,128)(2,1)}), bf16[4096,512]{1,0:T(8,128)(2,1)}) %all-gather.6.cloned.1.call-update) | async-done | bytes 4194320 | tf_op jit(solution)/shard_map/all_gather | solution.py:100
  44.6 3.4 %fusion.31 = bf16[256,512]{1,0:T(8,128)(2,1)S(1)} fusion(bf16[4096,512]{1,0:T(8,128)(2,1)} %all-gather.6.cloned.1.call-done, bf16[1,256,4096]{2,1,0:T(8,128)(2,1)S(1)} %copy-done), kind=kOutput, calls=%fused_computation.52 | convolution fusion | flops 1073872896 | bytes 6553600 | tf_op jit(solution)/shard_map/dot_general | solution.py:104
  48.0 1.3 collective-permute-start
  49.4 9.0 %collective-permute-done = bf16[256,512]{1,0:T(8,128)(2,1)S(1)} collective-permute-done((bf16[256,512]{1,0:T(8,128)(2,1)S(1)}, bf16[256,512]{1,0:T(8,128)(2,1)S(1)}, u32[]{:S(2)}, u32[]{:S(2)}) %collective-permute-start) | collective-permute-done | bytes 262176 | tf_op jit(solution)/shard_map/ppermute | solution.py:19
  59.2 21.4 %all-gather.12.cloned.1.call-done = bf16[4096,512]{1,0:T(8,128)(2,1)} async-done(((bf16[1024,512]{1,0:T(8,128)(2,1)}), bf16[4096,512]{1,0:T(8,128)(2,1)}) %all-gather.12.cloned.1.call-update) | async-done | bytes 4194320 | tf_op jit(solution)/shard_map/all_gather | solution.py:101
  80.7 3.4 %fusion.37 = bf16[256,512]{1,0:T(8,128)(2,1)S(1)} fusion(bf16[4096,512]{1,0:T(8,128)(2,1)} %all-gather.12.cloned.1.call-done, bf16[1,256,4096]{2,1,0:T(8,128)(2,1)S(1)} %copy-done), kind=kOutput, calls=%fused_computation.54 | convolution fusion | flops 1073872896 | bytes 6553600 | tf_op jit(solution)/shard_map/dot_general | solution.py:104
  84.1 1.3 collective-permute-start.1
  85.4 9.0 %collective-permute-done.1 = bf16[256,512]{1,0:T(8,128)(2,1)S(1)} collective-permute-done((bf16[256,512]{1,0:T(8,128)(2,1)S(1)}, bf16[256,512]{1,0:T(8,128)(2,1)S(1)}, u32[]{:S(2)}, u32[]{:S(2)}) %collective-permute-start.1) | collective-permute-done | bytes 262176 | tf_op jit(solution)/shard_map/ppermute | solution.py:19
  96.8 0.8 copy.58
  97.6 19.1 %all-gather.10.cloned.1.call-done = bf16[4096,512]{1,0:T(8,128)(2,1)} async-done(((bf16[1024,512]{1,0:T(8,128)(2,1)}), bf16[4096,512]{1,0:T(8,128)(2,1)}) %all-gather.10.cloned.1.call-update) | async-done | bytes 4194320 | tf_op jit(solution)/shard_map/all_gather | solution.py:99
  116.7 3.4 %fusion.34 = bf16[256,512]{1,0:T(8,128)(2,1)S(1)} fusion(bf16[4096,512]{1,0:T(8,128)(2,1)} %all-gather.10.cloned.1.call-done, bf16[1,256,4096]{2,1,0:T(8,128)(2,1)S(1)} %copy-done), kind=kOutput, calls=%fused_computation.53 | convolution fusion | flops 1073872896 | bytes 6553600 | tf_op jit(solution)/shard_map/dot_general | solution.py:104
  120.5 0.9 copy-done.3
  122.3 12.6 %all-gather.8.cloned.1.call-done = bf16[1024,512]{1,0:T(8,128)(2,1)} async-done(((bf16[256,512]{1,0:T(8,128)(2,1)}), bf16[1024,512]{1,0:T(8,128)(2,1)}) %all-gather.8.cloned.1.call-update) | async-done | bytes 1048592 | tf_op jit(solution)/shard_map/all_gather | solution.py:126
  134.9 18.1 %all-gather.14.cloned.1.call-done = bf16[1024,512]{1,0:T(8,128)(2,1)} async-done(((bf16[256,512]{1,0:T(8,128)(2,1)}), bf16[1024,512]{1,0:T(8,128)(2,1)}) %all-gather.14.cloned.1.call-update) | async-done | bytes 1048592 | tf_op jit(solution)/shard_map/all_gather | solution.py:127
  153.0 35.2 %while.17 = (s32[]{:T(128)}, f32[4,256]{1,0:T(4,128)S(1)}, f32[4,256]{1,0:T(4,128)S(1)}, f32[256,512]{0,1:T(8,128)}, pred[]{:T(512)}, /*index=5*/s32[2]{0:T(128)...) while((s32[]{:T(128)}, f32[4,256]{1,0:T(4,128)S(1)}, ...), condition=%wide.region_4.5_spmd.clone, body=%wide.region_0.4_spmd.clone.sunk | while | flops 278184192 | bytes 19628684 | solution.py:86
  154.3 1.4 compare_reduce_fusion.2
  158.9 1.5 constant_dynamic-slice_fusion.4
  160.4 1.0 copy.104
  161.4 2.9 %fusion.83 = (f32[4,256]{1,0:T(4,128)S(1)}, f32[4,512,256]{2,1,0:T(8,128)}) fusion(pred[256,512]{0,1:T(8,128)(4,1)S(1)} %copy.103, bf16[512,4,128]{0,2,1:T(8,128)(2,1)} %bitcast.145, bf16[256,512]{1,0:T(8,128)(2,1)S(1)} %get-tuple-element.412), kind=kOutput, calls=%fused_computation.4.clone.1 | convolution fusion | flops 135789568 | bytes 3018752 | tf_op jit(solution)/shard_map/while/body/eval_jaxpr/rhd,shd->hrs/dot_general | solution.py:28
  164.3 2.1 %fusion.85 = f32[4,256]{1,0:T(4,128)S(1)} fusion(f32[4,512,256]{2,1,0:T(8,128)} %get-tuple-element.368, f32[4,256]{1,0:T(4,128)S(1)} %get-tuple-element.366, pred[256,512]{0,1:T(8,128)(4,1)S(1)} %copy.103), kind=kLoop, calls=%fused_computation.6.clone.1 | loop fusion | flops 2620416 | bytes 2236416 | tf_op jit(solution)/shard_map/while/body/eval_jaxpr/reduce_sum | solution.py:34
  167.3 2.3 %fusion.87 = f32[256,4,128]{0,2,1:T(8,128)S(1)} fusion(bf16[512,4,128]{0,2,1:T(8,128)(2,1)S(1)} %bitcast.146, f32[4,512,256]{2,1,0:T(8,128)} %get-tuple-element.368, f32[4,256]{1,0:T(4,128)S(1)} %get-tuple-element.366, pred[256,512]{0,1:T(8,128)(4,1)S(1)} %copy.103, f32[256,4]{0,1:T(4,128)} %get-tuple-element.371), kind=kOutput, calls=%fused_computation.8.clone.1 | convolution fusion | flops 136970240 | bytes 3284992 | tf_op jit(solution)/shard_map/while/body/eval_jaxpr/hrs,shd->rhd/dot_general | solution.py:35
  169.8 0.8 copy-done.2
  171.9 1.4 compare_reduce_fusion.2
  176.6 1.5 constant_dynamic-slice_fusion.4
  178.0 1.0 copy.104
  179.0 2.9 %fusion.83 = (f32[4,256]{1,0:T(4,128)S(1)}, f32[4,512,256]{2,1,0:T(8,128)}) fusion(pred[256,512]{0,1:T(8,128)(4,1)S(1)} %copy.103, bf16[512,4,128]{0,2,1:T(8,128)(2,1)} %bitcast.145, bf16[256,512]{1,0:T(8,128)(2,1)S(1)} %get-tuple-element.412), kind=kOutput, calls=%fused_computation.4.clone.1 | convolution fusion | flops 135789568 | bytes 3018752 | tf_op jit(solution)/shard_map/while/body/eval_jaxpr/rhd,shd->hrs/dot_general | solution.py:28
  182.0 2.1 %fusion.85 = f32[4,256]{1,0:T(4,128)S(1)} fusion(f32[4,512,256]{2,1,0:T(8,128)} %get-tuple-element.368, f32[4,256]{1,0:T(4,128)S(1)} %get-tuple-element.366, pred[256,512]{0,1:T(8,128)(4,1)S(1)} %copy.103), kind=kLoop, calls=%fused_computation.6.clone.1 | loop fusion | flops 2620416 | bytes 2236416 | tf_op jit(solution)/shard_map/while/body/eval_jaxpr/reduce_sum | solution.py:34
  184.9 2.3 %fusion.87 = f32[256,4,128]{0,2,1:T(8,128)S(1)} fusion(bf16[512,4,128]{0,2,1:T(8,128)(2,1)S(1)} %bitcast.146, f32[4,512,256]{2,1,0:T(8,128)} %get-tuple-element.368, f32[4,256]{1,0:T(4,128)S(1)} %get-tuple-element.366, pred[256,512]{0,1:T(8,128)(4,1)S(1)} %copy.103, f32[256,4]{0,1:T(4,128)} %get-tuple-element.371), kind=kOutput, calls=%fused_computation.8.clone.1 | convolution fusion | flops 136970240 | bytes 3284992 | tf_op jit(solution)/shard_map/while/body/eval_jaxpr/hrs,shd->rhd/dot_general | solution.py:35
  188.2 1.2 copy.46
  190.5 2.4 %fusion.30 = f32[256,4,128]{0,2,1:T(8,128)} fusion(bf16[256,4,128]{0,2,1:T(8,128)(2,1)} %bitcast.151, f32[4,256,256]{1,2,0:T(8,128)} %copy-done.3, f32[4,256]{1,0:T(4,128)} %copy-done.5, pred[256,256]{0,1:T(8,128)(4,1)} %copy-done.4, f32[256,4]{0,1:T(4,128)S(1)} %get-tuple-element.274), kind=kOutput, calls=%fused_computation.51 | convolution fusion | flops 68026368 | bytes 1908736 | tf_op jit(solution)/shard_map/hrs,shd->rhd/dot_general | solution.py:35
  192.9 1.2 copy.59
  195.3 1.0 fusion.50
  (82 shorter events, 16.5 us)
Async XLA Ops:
  6.5 38.1 %copy-start = (bf16[1,256,4096]{2,1,0:T(8,128)(2,1)S(1)}, bf16[1,256,4096]{2,1,0:T(8,128)(2,1)}, u32[]{:S(2)}) copy-start(bf16[1,256,4096]{2,1,0:T(8,128)(2,1)} %param.8) | copy-start | bytes 6291460
  6.5 38.1 %all-gather.6.cloned.1.call-start = ((), (), s32[]{:S(2)}) async-start(), calls=%async_computation | async-start | bytes 5242880 | tf_op jit(solution)/shard_map/all_gather | solution.py:100
  7.3 73.4 %all-gather.12.cloned.1.call-start = ((), (), s32[]{:S(2)}) async-start(), calls=%async_computation.3 | async-start | bytes 5242880 | tf_op jit(solution)/shard_map/all_gather | solution.py:101
  8.0 108.7 %all-gather.10.cloned.1.call-start = ((), (), s32[]{:S(2)}) async-start(), calls=%async_computation.2 | async-start | bytes 5242880 | tf_op jit(solution)/shard_map/all_gather | solution.py:99
  8.7 126.1 %all-gather.8.cloned.1.call-start = ((), (), s32[]{:S(2)}) async-start(), calls=%async_computation.1 | async-start | bytes 1310720 | tf_op jit(solution)/shard_map/all_gather | solution.py:126
  48.0 10.3 %collective-permute-start = (bf16[256,512]{1,0:T(8,128)(2,1)S(1)}, bf16[256,512]{1,0:T(8,128)(2,1)S(1)}, u32[]{:S(2)}, u32[]{:S(2)}) collective-permute-start(bf16[256,512]{1,0:T(8,128)(2,1)S(1)} %fusion.31), channel_id=1, source_target_pairs={{0,16},{1,17},{2,18},{3,19},{4,20},{5,21},{6,22},{7,23},{8,24},{9,... | collective-permute-start | bytes 786440 | tf_op jit(solution)/shard_map/ppermute | solution.py:19
  59.1 36.1 %copy-start.6 = (s32[256,32]{0,1:T(8,128)S(1)}, s32[256,32]{0,1:T(8,128)}, u32[]{:S(2)}) copy-start(s32[256,32]{0,1:T(8,128)} %param.13) | copy-start | bytes 98308
  59.2 36.8 %copy-start.7 = (s32[256]{0:T(256)S(1)}, s32[256]{0:T(256)}, u32[]{:S(2)}) copy-start(s32[256]{0:T(256)} %param.12) | copy-start | bytes 3076
  59.2 93.8 %all-gather.14.cloned.1.call-start = ((), (), s32[]{:S(2)}) async-start(), calls=%async_computation.4 | async-start | bytes 1310720 | tf_op jit(solution)/shard_map/all_gather | solution.py:127
  84.1 10.3 %collective-permute-start.1 = (bf16[256,512]{1,0:T(8,128)(2,1)S(1)}, bf16[256,512]{1,0:T(8,128)(2,1)S(1)}, u32[]{:S(2)}, u32[]{:S(2)}) collective-permute-start(bf16[256,512]{1,0:T(8,128)(2,1)S(1)} %fusion.37), channel_id=1, source_target_pairs={{0,16},{1,17},{2,18},{3,19},{4,20},{5,21},{6,22},{7,23},{8,24},{9,... | collective-permute-start | bytes 786440 | tf_op jit(solution)/shard_map/ppermute | solution.py:19
  96.8 23.7 %copy-start.4 = (pred[256,256]{0,1:T(8,128)(4,1)}, pred[256,256]{0,1:T(8,128)(4,1)S(1)}, u32[]{:S(2)}) copy-start(pred[256,256]{0,1:T(8,128)(4,1)S(1)} %compare_and_fusion.1) | copy-start | bytes 196612
  120.5 1.0 copy-start.3
  120.5 32.5 %copy-start.5 = (f32[4,256]{1,0:T(4,128)}, f32[4,256]{1,0:T(4,128)S(1)}, u32[]{:S(2)}) copy-start(f32[4,256]{1,0:T(4,128)S(1)} %get-tuple-element.276) | copy-start | bytes 12292
  153.0 5.9 %copy-start.8 = (s32[2]{0:T(128)}, s32[2]{0:T(128)S(1)}, u32[]{:S(2)}) copy-start(s32[2]{0:T(128)S(1)} %get-tuple-element.408) | copy-start | bytes 28 | tf_op jit(solution)/shard_map/while
  167.3 2.4 %copy-start.1 = (f32[256,512]{0,1:T(8,128)S(1)}, f32[256,512]{0,1:T(8,128)}, u32[]{:S(2)}) copy-start(f32[256,512]{0,1:T(8,128)} %get-tuple-element.391) | copy-start | bytes 1572868 | tf_op jit(solution)/shard_map/while
  167.3 3.3 %copy-start.9 = (s32[2]{0:T(128)S(1)}, s32[2]{0:T(128)}, u32[]{:S(2)}) copy-start(s32[2]{0:T(128)} %copy-done.8) | copy-start | bytes 28 | tf_op jit(solution)/shard_map/while
  169.8 0.8 copy-start.2
  170.6 5.9 %copy-start.8 = (s32[2]{0:T(128)}, s32[2]{0:T(128)S(1)}, u32[]{:S(2)}) copy-start(s32[2]{0:T(128)S(1)} %get-tuple-element.408) | copy-start | bytes 28 | tf_op jit(solution)/shard_map/while
  184.9 2.4 %copy-start.1 = (f32[256,512]{0,1:T(8,128)S(1)}, f32[256,512]{0,1:T(8,128)}, u32[]{:S(2)}) copy-start(f32[256,512]{0,1:T(8,128)} %get-tuple-element.391) | copy-start | bytes 1572868 | tf_op jit(solution)/shard_map/while
  184.9 3.3 %copy-start.9 = (s32[2]{0:T(128)S(1)}, s32[2]{0:T(128)}, u32[]{:S(2)}) copy-start(s32[2]{0:T(128)} %copy-done.8) | copy-start | bytes 28 | tf_op jit(solution)/shard_map/while
  187.4 0.8 copy-start.2
Sparse Core Ops, SparseCore 0:
  8.9 35.6 all-gather.5
  46.2 34.4 all-gather.11
  82.2 34.4 all-gather.9
  118.1 16.6 all-gather.7
  136.3 16.6 all-gather.13
where the time goes:
time: 205 us; the launch traced here: 203 us
  waiting for transfers between devices  127 us (62%)
  matrix products  23.5 us (11%)
  local copies, waits for them, and re-layouts  16.1 us (8%)
  other arithmetic  15.7 us (8%)
  between operations  13.3 us (6%)
  loops' own time  4.12 us (2%)
  starting transfers between devices  2.74 us (1%)
    all_gather x1, waiting for transfers between devices, on_device(): lax.all_gather(w_key, 'seq', axis=0, tiled=True)  35.8 us
    all_gather x1, waiting for transfers between devices, on_device(): lax.all_gather(w_value, 'seq', axis=0, tiled=True)  21.4 us
    all_gather x1, waiting for transfers between devices, on_device(): lax.all_gather(w_query, 'seq', axis=0, tiled=True)  19.1 us
    all_gather x1, waiting for transfers between devices, on_device(): lax.all_gather(cache_values, 'seq', axis=0, tiled=True)  18.1 us
    ppermute x2, waiting for transfers between devices, from_behind(): lax.ppermute(value, axis, [(source, source + steps) for source in range(f...  18.1 us
    all_gather x1, waiting for transfers between devices, on_device(): lax.all_gather(cache_keys, 'seq', axis=0, tiled=True)  12.6 us
    dot_general x3, matrix products, on_device(): jnp.dot(local, weight, preferred_element_type=jnp.float32)  10.3 us
    dot_general x3, matrix products, partial_attention(): jnp.einsum('hrs,shd->rhd', weights.astype(jnp.bfloat16), value_heads, pre...  7.08 us
  transfers between devices with their start and end apart: 7, of which 7 were waited for; matrix products, arithmetic and copies ran while one was open for 7% of the time, Pallas kernels for 0%

commit v1 on v0

--- a/solution.py
+++ b/solution.py
@@ -3,6 +3,8 @@
 import jax
 import jax.numpy as jnp
 from jax import lax
+from jax.experimental import pallas as pl
+from jax.experimental.pallas import tpu as pltpu
 from jax.sharding import PartitionSpec as P
 
 HD = 128
@@ -137,9 +139,327 @@
     return jnp.where(is_prompt, prefill_out, decode_out)[None]
 
 
+QUERY, KEY, VALUE = 0, 1, 2
+ORDER = (KEY, VALUE, QUERY)
+SUBS = 2
+PARTS = 2
+
+
+def fused_kernel(
+    hidden, w_query, w_key, w_value, lengths, tables, out,
+    hbuf, near, far, acc, qbuf, fresh, cache, bias, osend, orecv,
+    y_send, y_recv, x_send, x_recv, d_send, d_recv, local_sem,
+    kx_send, kx_recv, ky_send, ky_recv, o_send, o_recv,
+):
+    weights = {QUERY: w_query, KEY: w_key, VALUE: w_value}
+    rows = hidden.shape[1]
+    depth = w_query.shape[0]
+    half = w_query.shape[1] // 2
+    heads = half // HD
+    chip_rows = 2 * rows
+    grp = lax.axis_index("grp")
+    seq = lax.axis_index("seq")
+    y = seq // 2
+    core = seq % 2
+    partner = {"seq": 2 * y + 1 - core}
+    across = [{"seq": 2 * (1 - y) + core}, {"seq": 2 * (1 - y) + 1 - core}]
+    beside = {"grp": 1 - grp}
+    core_of = [core, 1 - core]
+    piece = depth // 2 // SUBS
+
+    barrier = pltpu.get_barrier_semaphore()
+    for other in (partner, across[0], across[1], beside):
+        pl.semaphore_signal(barrier, inc=1, device_id=other, device_id_type=pl.DeviceIdType.MESH)
+    pl.semaphore_wait(barrier, 4)
+
+    def remote(src, dst, send, recv, to):
+        return pltpu.make_async_remote_copy(
+            src_ref=src, dst_ref=dst, send_sem=send, recv_sem=recv,
+            device_id=to, device_id_type=pl.DeviceIdType.MESH,
+        )
+
+    def columns(which):
+        return pl.ds(pl.multiple_of(core_of[which] * half, half), half)
+
+    steps = [(m, sub, rel) for m in ORDER for sub in range(SUBS) for rel in range(2)]
+
+    def slot(m, rel, way, sub):
+        return ((m * 2 + rel) * 2 + way) * SUBS + sub
+
+    def weight_copy(m, sub, rel):
+        first = pl.multiple_of(grp * (depth // 2) + sub * piece, piece)
+        at = slot(m, rel, 0, sub)
+        return remote(
+            weights[m].at[pl.ds(first, piece), columns(rel)],
+            far.at[at], y_send.at[at], y_recv.at[at], across[rel],
+        )
+
+    def forward_copy(m, sub, rel):
+        source, target = slot(m, rel, 0, sub), slot(m, rel, 1, sub)
+        return remote(far.at[source], far.at[target], x_send.at[target], x_recv.at[target], beside)
+
+    sent = []
+    for step in steps:
+        copy = weight_copy(*step)
+        copy.start()
+        sent.append(copy)
+    my_rows = pl.ds(pl.multiple_of(core * rows, rows), rows)
+    hidden_swap = remote(hidden.at[0], hbuf.at[my_rows], d_send.at[3], d_recv.at[3], partner)
+    hidden_swap.start()
+    swaps = {
+        m: remote(weights[m].at[:, columns(1)], near.at[2 * m + 1], d_send.at[m], d_recv.at[m], partner)
+        for m in ORDER
+    }
+    keeps = {
+        m: pltpu.make_async_copy(weights[m].at[:, columns(0)], near.at[2 * m], local_sem.at[m])
+        for m in ORDER
+    }
+    hidden_keep = pltpu.make_async_copy(hidden.at[0], hbuf.at[my_rows], local_sem.at[3])
+    hidden_keep.start()
+    for m in ORDER:
+        keeps[m].start()
+        swaps[m].start()
+    sent += [hidden_swap] + [swaps[m] for m in ORDER]
+
+    decode_rows = chip_rows // STEPS
+    all_rows = lengths.shape[1]
+    pages = 2 * chip_rows // PAGE
+    own_table = tables[pl.ds(pl.multiple_of(y * decode_rows, decode_rows), decode_rows), :]
+    page_lane = lax.broadcasted_iota(jnp.int32, (decode_rows, pages), 1)
+    member = own_table[:, 0:1] == page_lane
+    for listed in range(1, own_table.shape[1]):
+        member = member | (own_table[:, listed : listed + 1] == page_lane)
+    member = jnp.where(member, 1.0, 0.0).astype(jnp.bfloat16)
+    pick = (
+        lax.broadcasted_iota(jnp.int32, (decode_rows, all_rows), 1)
+        == lax.broadcasted_iota(jnp.int32, (decode_rows, all_rows), 0) + y * decode_rows
+    )
+    own_length = jnp.sum(jnp.where(pick, lengths[...], 0), axis=1, keepdims=True)
+    step_bits = STEPS.bit_length() - 1
+    page_bits = PAGE.bit_length() - 1
+    spread = (
+        lax.shift_right_logical(lax.broadcasted_iota(jnp.int32, (chip_rows, decode_rows), 0), step_bits)
+        == lax.broadcasted_iota(jnp.int32, (chip_rows, decode_rows), 1)
+    )
+    spread = jnp.where(spread, 1.0, 0.0).astype(jnp.bfloat16)
+    prompt_one = jnp.where(grp == 0, 1, 0)
+    for side in range(2):
+        base = (y if side == 0 else 1 - y) * chip_rows
+        key_page = lax.shift_right_logical(
+            lax.broadcasted_iota(jnp.int32, (pages, chip_rows), 1) + base, page_bits
+        )
+        unfold = lax.broadcasted_iota(jnp.int32, (pages, chip_rows), 0) == key_page
+        unfold = jnp.where(unfold, 1.0, 0.0).astype(jnp.bfloat16)
+        seen = jnp.dot(member, unfold, preferred_element_type=jnp.float32)
+        key_pos = lax.broadcasted_iota(jnp.int32, (decode_rows, chip_rows), 1) + base
+        seen = jnp.where(key_pos < own_length, seen, 0.0).astype(jnp.bfloat16)
+        listed = jnp.dot(spread, seen, preferred_element_type=jnp.float32)
+        causal = (
+            lax.broadcasted_iota(jnp.int32, (chip_rows, chip_rows), 1) + base
+            <= lax.broadcasted_iota(jnp.int32, (chip_rows, chip_rows), 0) + y * chip_rows
+        )
+        causal = jnp.where(causal, 1.0, 0.0)
+        allowed = jnp.where(prompt_one == 1, causal, listed)
+        bias[:, side * chip_rows : (side + 1) * chip_rows] = jnp.where(allowed > 0.5, 0.0, NEG)
+
+    def add(m, weight, first, count, fresh_start=False):
+        left = hbuf[:, pl.ds(pl.multiple_of(first, count), count)]
+        product = jnp.dot(left, weight, preferred_element_type=jnp.float32)
+        if fresh_start:
+            acc[m] = product
+        else:
+            acc[m] += product
+
+    hidden_keep.wait()
+    hidden_swap.wait_recv()
+    for m in ORDER:
+        keeps[m].wait()
+        add(m, near[2 * m], (2 * y + core) * depth, depth, True)
+        swaps[m].wait_recv()
+        add(m, near[2 * m + 1], (2 * y + 1 - core) * depth, depth)
+
+    def from_across(m, sub, rel, way):
+        owner = grp if way == 0 else 1 - grp
+        first = (2 * (1 - y) + core_of[rel]) * depth + owner * (depth // 2) + sub * piece
+        add(m, far[slot(m, rel, way, sub)], first, piece)
+
+    def take_y(step):
+        weight_copy(*step).wait_recv()
+        copy = forward_copy(*step)
+        copy.start()
+        sent.append(copy)
+        from_across(*step, 0)
+
+    def take_x(step):
+        forward_copy(*step).wait_recv()
+        from_across(*step, 1)
+
+    kv_steps = [step for step in steps if step[0] != QUERY]
+    q_steps = [step for step in steps if step[0] == QUERY]
+    lag = 2
+    for index, step in enumerate(kv_steps):
+        take_y(step)
+        if index >= lag:
+            take_x(kv_steps[index - lag])
+    for step in kv_steps[-lag:]:
+        take_x(step)
+
+    kv_pieces = [(kind, part) for kind in range(2) for part in range(PARTS)]
+    part_rows = chip_rows // PARTS
+
+    def piece_of(ref, at, part):
+        return ref.at[at, pl.ds(part * part_rows, part_rows)]
+
+    def kx_copy(kind, part):
+        at = kind * PARTS + part
+        return remote(
+            piece_of(fresh, kind, part), piece_of(cache, kind, part), kx_send.at[at], kx_recv.at[at], beside
+        )
+
+    def ky_copy(kind, part, source):
+        at = kind * PARTS + part
+        return remote(
+            piece_of(source, kind, part), piece_of(cache, 2 + kind, part),
+            ky_send.at[at], ky_recv.at[at], across[0],
+        )
+
+    fresh[0] = acc[KEY].astype(jnp.bfloat16)
+    fresh[1] = acc[VALUE].astype(jnp.bfloat16)
+
+    @pl.when(grp == 0)
+    def _():
+        for kind, part in kv_pieces:
+            kx_copy(kind, part).start()
+            ky_copy(kind, part, fresh).start()
+        cache[0] = acc[KEY].astype(jnp.bfloat16)
+        cache[1] = acc[VALUE].astype(jnp.bfloat16)
+
+    for step in q_steps:
+        take_y(step)
+
+    @pl.when(grp != 0)
+    def _():
+        for kind, part in kv_pieces:
+            kx_copy(kind, part).wait_recv()
+            ky_copy(kind, part, cache).start()
+
+    for step in q_steps:
+        take_x(step)
+    qbuf[...] = acc[QUERY].astype(jnp.bfloat16)
+    for kind, part in kv_pieces:
+        ky_copy(kind, part, cache).wait_recv()
+
+    block = min(rows, 128)
+    contract_last = (((1,), (1,)), ((), ()))
+    fresh_row = lax.broadcasted_iota(jnp.int32, (block, block), 0)
+    fresh_col = lax.broadcasted_iota(jnp.int32, (block, block), 1)
+    same = (
+        lax.shift_right_logical(fresh_row, step_bits) == lax.shift_right_logical(fresh_col, step_bits)
+    ) & (fresh_col <= fresh_row)
+    fresh_bias = jnp.where(jnp.where(same, 1 - prompt_one, 0) == 1, 0.0, NEG)
+    scale = HD ** (-0.5)
+
+    def attend(first, head):
+        span = pl.ds(pl.multiple_of(first, block), block)
+        lanes = slice(head * HD, (head + 1) * HD)
+        query = qbuf[span, lanes]
+
+        def scored(keys, mask):
+            return lax.dot_general(
+                query, keys, contract_last, preferred_element_type=jnp.float32
+            ) * scale + mask
+
+        scores = [
+            scored(cache[0, :, lanes], bias[span, 0:chip_rows]),
+            scored(cache[2, :, lanes], bias[span, chip_rows : 2 * chip_rows]),
+            scored(fresh[0, span, lanes], fresh_bias),
+        ]
+        values = [cache[1, :, lanes], cache[3, :, lanes], fresh[1, span, lanes]]
+        top = jnp.maximum(
+            jnp.maximum(
+                jnp.max(scores[0], axis=1, keepdims=True), jnp.max(scores[1], axis=1, keepdims=True)
+            ),
+            jnp.max(scores[2], axis=1, keepdims=True),
+        )
+        total = jnp.zeros((block, 1), jnp.float32)
+        summed = jnp.zeros((block, HD), jnp.float32)
+        for score, value in zip(scores, values):
+            weight = jnp.exp(score - top)
+            total += jnp.sum(weight, axis=1, keepdims=True)
+            summed += jnp.dot(weight.astype(jnp.bfloat16), value, preferred_element_type=jnp.float32)
+        return (summed / total).astype(jnp.bfloat16)
+
+    for at in range(rows // block):
+        for head in range(heads):
+            osend[at * block : (at + 1) * block, head * HD : (head + 1) * HD] = attend(
+                (1 - core) * rows + at * block, head
+            )
+    swap_out = remote(osend, orecv, o_send, o_recv, partner)
+    swap_out.start()
+    for at in range(rows // block):
+        for head in range(heads):
+            out[at * block : (at + 1) * block, pl.ds(pl.multiple_of(core * half + head * HD, HD), HD)] = attend(
+                core * rows + at * block, head
+            )
+    swap_out.wait()
+    out[:, columns(1)] = orecv[...]
+
+    for copy in sent:
+        copy.wait_send()
+
+    @pl.when(grp == 0)
+    def _():
+        for kind, part in kv_pieces:
+            kx_copy(kind, part).wait_send()
+            ky_copy(kind, part, fresh).wait_send()
+
+    @pl.when(grp != 0)
+    def _():
+        for kind, part in kv_pieces:
+            ky_copy(kind, part, cache).wait_send()
+
+
+def fused(hidden, w_query, w_key, w_value, prompt_len, page_table):
+    rows, model = hidden.shape[1:]
+    depth, width = w_query.shape
+    half = width // 2
+    chip_rows = 2 * rows
+    slots = 3 * 2 * 2 * SUBS
+    dma = pltpu.SemaphoreType.DMA
+    anywhere = pl.BlockSpec(memory_space=pl.ANY)
+    vmem = pl.BlockSpec(memory_space=pltpu.VMEM)
+    result = pl.pallas_call(
+        fused_kernel,
+        out_shape=jax.ShapeDtypeStruct((rows, width), jnp.bfloat16),
+        in_specs=[anywhere] * 4 + [vmem] * 2,
+        out_specs=vmem,
+        scratch_shapes=[
+            pltpu.VMEM((chip_rows, model), jnp.bfloat16),
+            pltpu.VMEM((6, depth, half), jnp.bfloat16),
+            pltpu.VMEM((slots, depth // 2 // SUBS, half), jnp.bfloat16),
+            pltpu.VMEM((3, chip_rows, half), jnp.float32),
+            pltpu.VMEM((chip_rows, half), jnp.bfloat16),
+            pltpu.VMEM((2, chip_rows, half), jnp.bfloat16),
+            pltpu.VMEM((4, chip_rows, half), jnp.bfloat16),
+            pltpu.VMEM((chip_rows, 2 * chip_rows), jnp.float32),
+            pltpu.VMEM((rows, half), jnp.bfloat16),
+            pltpu.VMEM((rows, half), jnp.bfloat16),
+            dma((slots,)), dma((slots,)), dma((slots,)), dma((slots,)),
+            dma((4,)), dma((4,)), dma((4,)),
+            dma((2 * PARTS,)), dma((2 * PARTS,)), dma((2 * PARTS,)), dma((2 * PARTS,)),
+            dma, dma,
+        ],
+        compiler_params=pltpu.CompilerParams(
+            collective_id=0, has_side_effects=True, vmem_limit_bytes=48 * 1024 * 1024
+        ),
+    )(hidden, w_query, w_key, w_value, prompt_len.reshape(1, -1), page_table)
+    return result[None]
+
+
 def solution(mesh):
+    paired = mesh.shape["grp"] == 2 and mesh.shape["seq"] == 4
     return jax.shard_map(
-        on_device,
+        fused if paired else on_device,
         mesh=mesh,
         in_specs=(P("grp", "seq", None), P("seq", "tp"), P("seq", "tp"), P("seq", "tp"), P(), P()),
         out_specs=P("grp", "seq", "tp"),

time: 205 us -> 71.7 us (0.35)
  waiting for transfers between devices: 127 us -> 0 us
  Pallas kernels: 0 us -> 63.9 us
  matrix products: 23.5 us -> 0 us
  other arithmetic: 15.7 us -> 0 us
  between operations: 13.3 us -> 0.02 us
  local copies, waits for them, and re-layouts: 16.1 us -> 7.5 us
  loops' own time: 4.12 us -> 0 us
  starting transfers between devices: 2.74 us -> 0 us
    all_gather x5 -> x0, waiting for transfers between devices: 107 us -> none  [the longest x1 35.8 us: on_device(): lax.all_gather(w_key, 'seq', axis=0, tiled=True)]
    pallas_call x0 -> x1, Pallas kernels: none -> 63.9 us  [fused(): pl.pallas_call(fused_kernel, out_shape=jax.ShapeDtypeStruct((rows, width)...]
    dot_general x9 -> x0, matrix products: 23.5 us -> none  [the longest x3 10.3 us: on_device(): jnp.dot(local, weight, preferred_element_type=jnp.float32)]
    ppermute x2 -> x0, waiting for transfers between devices: 18.1 us -> none  [from_behind(): lax.ppermute(value, axis, [(source, source + steps) for source in range(f...]
    dynamic_slice x10 -> x0, local copies, waits for them, and re-layouts: 7.16 us -> none  [the longest x4 3.33 us: one_block(): piece_values = lax.dynamic_slice_in_dim(values, offset, block, 0)]
    unnamed x13 -> x12, local copies, waits for them, and re-layouts: 1.67 us -> 7.5 us
    reduce_sum x3 -> x0, other arithmetic: 5.04 us -> none  [partial_attention(): total = jnp.sum(weights, axis=2)]
    another operation x1 -> x0, loops' own time: 4.12 us -> none  [blocked(): state, unused = lax.scan(one_block, carry, offsets)]
  transfers between devices with their start and end apart: 7 -> 0, of which waited for: 7 -> 0; matrix products, arithmetic and copies ran while one was open for 7% -> 0% of each run, Pallas kernels for 0% -> 0%
where the time goes in v1:
time: 71.7 us; the launch traced here: 71.4 us
  Pallas kernels  63.9 us (89%)
  local copies, waits for them, and re-layouts  7.5 us (10%)
    pallas_call x1, Pallas kernels, fused(): pl.pallas_call(fused_kernel, out_shape=jax.ShapeDtypeStruct((rows, width)...  63.9 us
    unnamed x12, local copies, waits for them, and re-layouts  7.5 us

profile of v1, /device:TPU:2, one launch (start us, length us, event | category | flops | bytes accessed | tf_op | source)
XLA Modules:
  0.0 71.4 jit_solution(16544052863031391527)
XLA Ops:
  0.0 0.9 %copy.7.tables = s32[256,32]{1,0:T(8,128)S(1)} copy(s32[256,32]{0,1:T(8,128)} %param.11) | data formatting | bytes 65536 | tf_op args[5]
  0.9 0.0 copy-start
  0.9 1.6 %copy-done = bf16[1,256,4096]{2,1,0:T(8,128)(2,1)S(1)} copy-done((bf16[1,256,4096]{2,1,0:T(8,128)(2,1)S(1)}, bf16[1,256,4096]{2,1,0:T(8,128)(2,1)}, u32[]{:S(2)}) %copy-start) | copy-done | bytes 2097176
  2.5 0.0 copy-start.1
  2.5 1.2 %copy-done.1 = bf16[1024,512]{1,0:T(8,128)(2,1)S(1)} copy-done((bf16[1024,512]{1,0:T(8,128)(2,1)S(1)}, bf16[1024,512]{1,0:T(8,128)(2,1)}, u32[]{:S(2)}) %copy-start.1) | copy-done | bytes 1048600
  3.7 0.0 copy-start.2
  3.7 1.2 %copy-done.2 = bf16[1024,512]{1,0:T(8,128)(2,1)S(1)} copy-done((bf16[1024,512]{1,0:T(8,128)(2,1)S(1)}, bf16[1024,512]{1,0:T(8,128)(2,1)}, u32[]{:S(2)}) %copy-start.2) | copy-done | bytes 1048600
  4.9 0.0 copy-start.3
  4.9 1.2 %copy-done.3 = bf16[1024,512]{1,0:T(8,128)(2,1)S(1)} copy-done((bf16[1024,512]{1,0:T(8,128)(2,1)S(1)}, bf16[1024,512]{1,0:T(8,128)(2,1)}, u32[]{:S(2)}) %copy-start.3) | copy-done | bytes 1048600
  6.1 0.0 copy-start.4
  6.1 0.7 copy-done.4
  6.8 63.9 %shard_map.64 = bf16[256,512]{1,0:T(8,128)(2,1)S(1)} custom-call(bf16[1,256,4096]{2,1,0:T(8,128)(2,1)S(1)} %copy-done, bf16[1024,512]{1,0:T(8,128)(2,1)S(1)} %copy-done.1, bf16[1024,512]{1,0:T(8,128)(2,1)S(1)} %copy-done.2, bf16[1024,512]{1,0:T(8,128)(2,1)S(1)} %copy-done.3, s32[1,256]{1,0:T(1,128)S(1)} %bitcast.3, s32[256,32]{1,0:T(8,128)S(1)} %copy.7.tables), custom_call_target="tpu_custom_call" | custom-call | tf_op jit(solution)/shard_map/pallas_call | solution.py:431
  70.7 0.7 copy.9
Async XLA Ops:
  0.9 1.6 %copy-start = (bf16[1,256,4096]{2,1,0:T(8,128)(2,1)S(1)}, bf16[1,256,4096]{2,1,0:T(8,128)(2,1)}, u32[]{:S(2)}) copy-start(bf16[1,256,4096]{2,1,0:T(8,128)(2,1)} %hidden.1) | copy-start | bytes 6291460
  2.5 1.2 %copy-start.1 = (bf16[1024,512]{1,0:T(8,128)(2,1)S(1)}, bf16[1024,512]{1,0:T(8,128)(2,1)}, u32[]{:S(2)}) copy-start(bf16[1024,512]{1,0:T(8,128)(2,1)} %w_query.1) | copy-start | bytes 3145732
  3.7 1.2 %copy-start.2 = (bf16[1024,512]{1,0:T(8,128)(2,1)S(1)}, bf16[1024,512]{1,0:T(8,128)(2,1)}, u32[]{:S(2)}) copy-start(bf16[1024,512]{1,0:T(8,128)(2,1)} %w_key.1) | copy-start | bytes 3145732
  4.9 1.2 %copy-start.3 = (bf16[1024,512]{1,0:T(8,128)(2,1)S(1)}, bf16[1024,512]{1,0:T(8,128)(2,1)}, u32[]{:S(2)}) copy-start(bf16[1024,512]{1,0:T(8,128)(2,1)} %w_value.1) | copy-start | bytes 3145732
  6.1 0.7 copy-start.4

commit v2 on v1

--- a/solution.py
+++ b/solution.py
@@ -141,13 +141,14 @@
 
 QUERY, KEY, VALUE = 0, 1, 2
 ORDER = (KEY, VALUE, QUERY)
-SUBS = 2
+SUBS = 1
+LAG = 1
 PARTS = 2
 
 
 def fused_kernel(
-    hidden, w_query, w_key, w_value, lengths, tables, out,
-    hbuf, near, far, acc, qbuf, fresh, cache, bias, osend, orecv,
+    hidden, w_query, w_key, w_value, lengths_in, tables_in, out,
+    lengths, tables, hbuf, near, far, far_q, acc, qbuf, fresh, cache, bias, osend, orecv,
     y_send, y_recv, x_send, x_recv, d_send, d_recv, local_sem,
     kx_send, kx_recv, ky_send, ky_recv, o_send, o_recv,
 ):
@@ -181,22 +182,39 @@
     def columns(which):
         return pl.ds(pl.multiple_of(core_of[which] * half, half), half)
 
-    steps = [(m, sub, rel) for m in ORDER for sub in range(SUBS) for rel in range(2)]
+    kv_steps = [(m, sub, rel) for m in (KEY, VALUE) for sub in range(SUBS) for rel in range(2)]
+    q_steps = [(QUERY, head, rel) for head in range(heads) for rel in range(2)]
+    steps = kv_steps + q_steps
 
     def slot(m, rel, way, sub):
-        return ((m * 2 + rel) * 2 + way) * SUBS + sub
+        if m == QUERY:
+            return (sub * 2 + rel) * 2 + way
+        return (((m - KEY) * SUBS + sub) * 2 + rel) * 2 + way
+
+    def landing(m, rel, way, sub):
+        return (far_q if m == QUERY else far).at[slot(m, rel, way, sub)]
+
+    def number(m, rel, way, sub):
+        return slot(m, rel, way, sub) + (8 * SUBS if m == QUERY else 0)
 
     def weight_copy(m, sub, rel):
-        first = pl.multiple_of(grp * (depth // 2) + sub * piece, piece)
-        at = slot(m, rel, 0, sub)
+        if m == QUERY:
+            span = pl.ds(pl.multiple_of(grp * (depth // 2), depth // 2), depth // 2)
+            across_lanes = pl.ds(pl.multiple_of(core_of[rel] * half + sub * HD, HD), HD)
+        else:
+            span = pl.ds(pl.multiple_of(grp * (depth // 2) + sub * piece, piece), piece)
+            across_lanes = columns(rel)
+        at = number(m, rel, 0, sub)
         return remote(
-            weights[m].at[pl.ds(first, piece), columns(rel)],
-            far.at[at], y_send.at[at], y_recv.at[at], across[rel],
+            weights[m].at[span, across_lanes], landing(m, rel, 0, sub),
+            y_send.at[at], y_recv.at[at], across[rel],
         )
 
     def forward_copy(m, sub, rel):
-        source, target = slot(m, rel, 0, sub), slot(m, rel, 1, sub)
-        return remote(far.at[source], far.at[target], x_send.at[target], x_recv.at[target], beside)
+        at = number(m, rel, 1, sub)
+        return remote(
+            landing(m, rel, 0, sub), landing(m, rel, 1, sub), x_send.at[at], x_recv.at[at], beside
+        )
 
     sent = []
     for step in steps:
@@ -221,20 +239,23 @@
         swaps[m].start()
     sent += [hidden_swap] + [swaps[m] for m in ORDER]
 
+    table_keep = pltpu.make_async_copy(tables_in, tables, local_sem.at[4])
+    length_keep = pltpu.make_async_copy(lengths_in, lengths, local_sem.at[5])
+    table_keep.start()
+    length_keep.start()
+    table_keep.wait()
+    length_keep.wait()
+
     decode_rows = chip_rows // STEPS
-    all_rows = lengths.shape[1]
     pages = 2 * chip_rows // PAGE
-    own_table = tables[pl.ds(pl.multiple_of(y * decode_rows, decode_rows), decode_rows), :]
-    page_lane = lax.broadcasted_iota(jnp.int32, (decode_rows, pages), 1)
-    member = own_table[:, 0:1] == page_lane
-    for listed in range(1, own_table.shape[1]):
-        member = member | (own_table[:, listed : listed + 1] == page_lane)
+    own_rows = pl.ds(pl.multiple_of(y * decode_rows, decode_rows), decode_rows)
+    own_table = tables[:, own_rows]
+    own_length = lengths[:, own_rows]
+    page_row = lax.broadcasted_iota(jnp.int32, (pages, decode_rows), 0)
+    member = own_table[0:1, :] == page_row
+    for listed in range(1, own_table.shape[0]):
+        member = member | (own_table[listed : listed + 1, :] == page_row)
     member = jnp.where(member, 1.0, 0.0).astype(jnp.bfloat16)
-    pick = (
-        lax.broadcasted_iota(jnp.int32, (decode_rows, all_rows), 1)
-        == lax.broadcasted_iota(jnp.int32, (decode_rows, all_rows), 0) + y * decode_rows
-    )
-    own_length = jnp.sum(jnp.where(pick, lengths[...], 0), axis=1, keepdims=True)
     step_bits = STEPS.bit_length() - 1
     page_bits = PAGE.bit_length() - 1
     spread = (
@@ -243,17 +264,18 @@
     )
     spread = jnp.where(spread, 1.0, 0.0).astype(jnp.bfloat16)
     prompt_one = jnp.where(grp == 0, 1, 0)
+    contract_last = (((1,), (1,)), ((), ()))
     for side in range(2):
         base = (y if side == 0 else 1 - y) * chip_rows
         key_page = lax.shift_right_logical(
-            lax.broadcasted_iota(jnp.int32, (pages, chip_rows), 1) + base, page_bits
-        )
-        unfold = lax.broadcasted_iota(jnp.int32, (pages, chip_rows), 0) == key_page
+            lax.broadcasted_iota(jnp.int32, (chip_rows, pages), 0) + base, page_bits
+        )
+        unfold = lax.broadcasted_iota(jnp.int32, (chip_rows, pages), 1) == key_page
         unfold = jnp.where(unfold, 1.0, 0.0).astype(jnp.bfloat16)
-        seen = jnp.dot(member, unfold, preferred_element_type=jnp.float32)
-        key_pos = lax.broadcasted_iota(jnp.int32, (decode_rows, chip_rows), 1) + base
+        seen = jnp.dot(unfold, member, preferred_element_type=jnp.float32)
+        key_pos = lax.broadcasted_iota(jnp.int32, (chip_rows, decode_rows), 0) + base
         seen = jnp.where(key_pos < own_length, seen, 0.0).astype(jnp.bfloat16)
-        listed = jnp.dot(spread, seen, preferred_element_type=jnp.float32)
+        listed = lax.dot_general(spread, seen, contract_last, preferred_element_type=jnp.float32)
         causal = (
             lax.broadcasted_iota(jnp.int32, (chip_rows, chip_rows), 1) + base
             <= lax.broadcasted_iota(jnp.int32, (chip_rows, chip_rows), 0) + y * chip_rows
@@ -280,8 +302,15 @@
 
     def from_across(m, sub, rel, way):
         owner = grp if way == 0 else 1 - grp
-        first = (2 * (1 - y) + core_of[rel]) * depth + owner * (depth // 2) + sub * piece
-        add(m, far[slot(m, rel, way, sub)], first, piece)
+        first = (2 * (1 - y) + core_of[rel]) * depth + owner * (depth // 2)
+        weight = landing(m, rel, way, sub)[...]
+        if m != QUERY:
+            add(m, weight, first + sub * piece, piece)
+            return
+        left = hbuf[:, pl.ds(pl.multiple_of(first, depth // 2), depth // 2)]
+        acc[m, :, sub * HD : (sub + 1) * HD] += jnp.dot(
+            left, weight, preferred_element_type=jnp.float32
+        )
 
     def take_y(step):
         weight_copy(*step).wait_recv()
@@ -294,16 +323,6 @@
         forward_copy(*step).wait_recv()
         from_across(*step, 1)
 
-    kv_steps = [step for step in steps if step[0] != QUERY]
-    q_steps = [step for step in steps if step[0] == QUERY]
-    lag = 2
-    for index, step in enumerate(kv_steps):
-        take_y(step)
-        if index >= lag:
-            take_x(kv_steps[index - lag])
-    for step in kv_steps[-lag:]:
-        take_x(step)
-
     kv_pieces = [(kind, part) for kind in range(2) for part in range(PARTS)]
     part_rows = chip_rows // PARTS
 
@@ -323,18 +342,27 @@
             ky_send.at[at], ky_recv.at[at], across[0],
         )
 
-    fresh[0] = acc[KEY].astype(jnp.bfloat16)
-    fresh[1] = acc[VALUE].astype(jnp.bfloat16)
-
-    @pl.when(grp == 0)
-    def _():
-        for kind, part in kv_pieces:
-            kx_copy(kind, part).start()
-            ky_copy(kind, part, fresh).start()
-        cache[0] = acc[KEY].astype(jnp.bfloat16)
-        cache[1] = acc[VALUE].astype(jnp.bfloat16)
-
-    for step in q_steps:
+    def settle(kind, m):
+        fresh[kind] = acc[m].astype(jnp.bfloat16)
+
+        @pl.when(grp == 0)
+        def _():
+            for part in range(PARTS):
+                kx_copy(kind, part).start()
+                ky_copy(kind, part, fresh).start()
+            cache[kind] = acc[m].astype(jnp.bfloat16)
+
+    lag = LAG
+    settled = {(KEY, SUBS - 1, 1): (0, KEY), (VALUE, SUBS - 1, 1): (1, VALUE)}
+    for index in range(len(kv_steps) + lag):
+        take_y(steps[index])
+        if index >= lag:
+            step = steps[index - lag]
+            take_x(step)
+            if step in settled:
+                settle(*settled[step])
+
+    for step in q_steps[lag:]:
         take_y(step)
 
     @pl.when(grp != 0)
@@ -343,14 +371,7 @@
             kx_copy(kind, part).wait_recv()
             ky_copy(kind, part, cache).start()
 
-    for step in q_steps:
-        take_x(step)
-    qbuf[...] = acc[QUERY].astype(jnp.bfloat16)
-    for kind, part in kv_pieces:
-        ky_copy(kind, part, cache).wait_recv()
-
     block = min(rows, 128)
-    contract_last = (((1,), (1,)), ((), ()))
     fresh_row = lax.broadcasted_iota(jnp.int32, (block, block), 0)
     fresh_col = lax.broadcasted_iota(jnp.int32, (block, block), 1)
     same = (
@@ -389,20 +410,26 @@
             summed += jnp.dot(weight.astype(jnp.bfloat16), value, preferred_element_type=jnp.float32)
         return (summed / total).astype(jnp.bfloat16)
 
-    for at in range(rows // block):
-        for head in range(heads):
-            osend[at * block : (at + 1) * block, head * HD : (head + 1) * HD] = attend(
-                (1 - core) * rows + at * block, head
-            )
-    swap_out = remote(osend, orecv, o_send, o_recv, partner)
-    swap_out.start()
-    for at in range(rows // block):
-        for head in range(heads):
-            out[at * block : (at + 1) * block, pl.ds(pl.multiple_of(core * half + head * HD, HD), HD)] = attend(
-                core * rows + at * block, head
-            )
-    swap_out.wait()
-    out[:, columns(1)] = orecv[...]
+    swaps_out = []
+    for head in range(heads):
+        lanes = slice(head * HD, (head + 1) * HD)
+        for rel in range(2):
+            take_x((QUERY, head, rel))
+        qbuf[:, lanes] = acc[QUERY, :, lanes].astype(jnp.bfloat16)
+        if head == 0:
+            for kind, part in kv_pieces:
+                ky_copy(kind, part, cache).wait_recv()
+        for at in range(rows // block):
+            osend[head, at * block : (at + 1) * block] = attend((1 - core) * rows + at * block, head)
+        swap_out = remote(osend.at[head], orecv.at[head], o_send.at[head], o_recv.at[head], partner)
+        swap_out.start()
+        swaps_out.append(swap_out)
+        for at in range(rows // block):
+            own_lanes = pl.ds(pl.multiple_of(core * half + head * HD, HD), HD)
+            out[at * block : (at + 1) * block, own_lanes] = attend(core * rows + at * block, head)
+    for head, swap_out in enumerate(swaps_out):
+        swap_out.wait()
+        out[:, pl.ds(pl.multiple_of((1 - core) * half + head * HD, HD), HD)] = orecv[head]
 
     for copy in sent:
         copy.wait_send()
@@ -424,35 +451,39 @@
     depth, width = w_query.shape
     half = width // 2
     chip_rows = 2 * rows
-    slots = 3 * 2 * 2 * SUBS
+    heads = half // HD
+    copies = 8 * SUBS + 4 * heads
     dma = pltpu.SemaphoreType.DMA
-    anywhere = pl.BlockSpec(memory_space=pl.ANY)
+    anywhere = pl.BlockSpec(memory_space=pltpu.HBM)
     vmem = pl.BlockSpec(memory_space=pltpu.VMEM)
     result = pl.pallas_call(
         fused_kernel,
         out_shape=jax.ShapeDtypeStruct((rows, width), jnp.bfloat16),
-        in_specs=[anywhere] * 4 + [vmem] * 2,
+        in_specs=[anywhere] * 6,
         out_specs=vmem,
         scratch_shapes=[
+            pltpu.VMEM((1, prompt_len.shape[0]), jnp.int32),
+            pltpu.VMEM(page_table.shape[::-1], jnp.int32),
             pltpu.VMEM((chip_rows, model), jnp.bfloat16),
             pltpu.VMEM((6, depth, half), jnp.bfloat16),
-            pltpu.VMEM((slots, depth // 2 // SUBS, half), jnp.bfloat16),
+            pltpu.VMEM((8 * SUBS, depth // 2 // SUBS, half), jnp.bfloat16),
+            pltpu.VMEM((4 * heads, depth // 2, HD), jnp.bfloat16),
             pltpu.VMEM((3, chip_rows, half), jnp.float32),
             pltpu.VMEM((chip_rows, half), jnp.bfloat16),
             pltpu.VMEM((2, chip_rows, half), jnp.bfloat16),
             pltpu.VMEM((4, chip_rows, half), jnp.bfloat16),
             pltpu.VMEM((chip_rows, 2 * chip_rows), jnp.float32),
-            pltpu.VMEM((rows, half), jnp.bfloat16),
-            pltpu.VMEM((rows, half), jnp.bfloat16),
-            dma((slots,)), dma((slots,)), dma((slots,)), dma((slots,)),
-            dma((4,)), dma((4,)), dma((4,)),
+            pltpu.VMEM((heads, rows, HD), jnp.bfloat16),
+            pltpu.VMEM((heads, rows, HD), jnp.bfloat16),
+            dma((copies,)), dma((copies,)), dma((copies,)), dma((copies,)),
+            dma((4,)), dma((4,)), dma((6,)),
             dma((2 * PARTS,)), dma((2 * PARTS,)), dma((2 * PARTS,)), dma((2 * PARTS,)),
-            dma, dma,
+            dma((heads,)), dma((heads,)),
         ],
         compiler_params=pltpu.CompilerParams(
-            collective_id=0, has_side_effects=True, vmem_limit_bytes=48 * 1024 * 1024
+            collective_id=0, has_side_effects=True, vmem_limit_bytes=67043328
         ),
-    )(hidden, w_query, w_key, w_value, prompt_len.reshape(1, -1), page_table)
+    )(hidden, w_query, w_key, w_value, prompt_len.reshape(1, -1), page_table.T)
     return result[None]
 
 

time: 71.7 us -> 62.5 us (0.87)
  local copies, waits for them, and re-layouts: 7.5 us -> 1.67 us
  Pallas kernels: 63.9 us -> 60.2 us
    unnamed x12 -> x1, local copies, waits for them, and re-layouts: 7.5 us -> 1.67 us
    pallas_call x1, Pallas kernels: 63.9 us -> 60.2 us  [fused(): pl.pallas_call(fused_kernel, out_shape=jax.ShapeDtypeStruct((rows, width)...]
where the time goes in v2:
time: 62.5 us; the launch traced here: 61.9 us
  Pallas kernels  60.2 us (96%)
  local copies, waits for them, and re-layouts  1.67 us (3%)
    pallas_call x1, Pallas kernels, fused(): pl.pallas_call(fused_kernel, out_shape=jax.ShapeDtypeStruct((rows, width)...  60.2 us
    unnamed x1, local copies, waits for them, and re-layouts  1.67 us

profile of v2, /device:TPU:2, one launch (start us, length us, event | category | flops | bytes accessed | tf_op | source)
XLA Modules:
  0.0 61.9 jit_solution(6668674086821506893)
XLA Ops:
  0.0 60.2 %shard_map.64 = bf16[256,512]{1,0:T(8,128)(2,1)} custom-call(bf16[1,256,4096]{2,1,0:T(8,128)(2,1)} %hidden.1, bf16[1024,512]{1,0:T(8,128)(2,1)} %w_query.1, bf16[1024,512]{1,0:T(8,128)(2,1)} %w_key.1, bf16[1024,512]{1,0:T(8,128)(2,1)} %w_value.1, s32[1,256]{1,0:T(1,128)} %bitcast.5, s32[32,256]{1,0:T(8,128)} %bitcast.4), custom_call_target="tpu_custom_call" | custom-call | tf_op jit(solution)/shard_map/pallas_call | solution.py:459
  60.2 1.7 %copy.8 = bf16[1,256,512]{2,1,0:T(8,128)(2,1)} copy(bf16[1,256,512]{2,1,0:T(8,128)(2,1)} %bitcast.3) | data formatting | bytes 524288
